TPU v7x, 32 devices: a whole 2x2x4 slice. The times are simulated.
32 devices in a mesh: peer: 8 (over y, x, core), zero: 4 (over z).
Axes of the slice: x: 2, y: 2, z: 4, core: 2. Of those that a mesh axis runs over, the one named last changes fastest.
Arguments:
- tokens: bfloat16 [8, 2048, 1024], P('peer', 'zero'), may hold values from -6 to 6
- out_grad: bfloat16 [8, 2048, 1024], P('peer', 'zero'), may hold values from -6 to 6
- step: int32 [1], replicated, may hold values from 0 to 3999
- up_param: float32 [8, 1024, 2048], P('peer', 'zero'), may hold values from -0.2 to 0.2
- down_param: float32 [8, 2048, 1024], P('peer', 'zero'), may hold values from -0.2 to 0.2
- up_first: float32 [8, 1024, 2048], P('peer', 'zero'), may hold values from -27.1529 to 27.1529
- down_first: float32 [8, 2048, 1024], P('peer', 'zero'), may hold values from -27.1529 to 27.1529
- up_second: float32 [8, 1024, 2048], P('peer', 'zero'), may hold values from 0.8192 to 819.2
- down_second: float32 [8, 2048, 1024], P('peer', 'zero'), may hold values from 0.8192 to 819.2
Outputs:
- new_up: float32 [8, 1024, 2048], P('peer', 'zero')
- new_down: float32 [8, 2048, 1024], P('peer', 'zero')
- new_up_first: float32 [8, 1024, 2048], P('peer', 'zero')
- new_down_first: float32 [8, 2048, 1024], P('peer', 'zero')
- new_up_second: float32 [8, 1024, 2048], P('peer', 'zero')
- new_down_second: float32 [8, 2048, 1024], P('peer', 'zero')
All inputs are finite; a program needn't handle non-finite values.
Results may differ from a plain program's by a relative error of at most 0.0065.
Values may be sent and summed in bfloat16 or wider, within the bound.
A program may use at most 128 MiB of HBM per device.

v0:
```python
from functools import partial

import jax
import jax.numpy as jnp
from jax import lax
from jax.experimental import pallas as pl
from jax.experimental.pallas import tpu as pltpu
from jax.sharding import PartitionSpec as P

MIB = 2**20
BF16, F32 = jnp.bfloat16, jnp.float32
EARLY = 1


def step_kernel(
    dist,
    dims,
    fixes,
    tok_in,
    out_in,
    up_in,
    down_in,
    up_first_in,
    down_first_in,
    up_second_in,
    down_second_in,
    up,
    down,
    up_first,
    down_first,
    up_second,
    down_second,
    toks,
    outs,
    normed,
    normed_t,
    up_stage,
    down_stage,
    up_cols,
    down_rows,
    act_t,
    pre_grad,
    up_grad,
    down_grad,
    up_got,
    down_got,
    up_mine,
    down_mine,
    up_other,
    down_other,
    load_sem,
    tok_send,
    tok_recv,
    fwd_send,
    upw_send,
    upw_recv,
    downw_send,
    downw_recv,
    upg_send,
    upg_recv,
    downg_send,
    downg_recv,
    upl_send,
    upl_recv,
    downl_send,
    downl_recv,
):
    n, tokens, width, units, unit_block, chunk = dims
    half = n // 2
    rows = width // n
    owned = units // n
    per_owner = owned // unit_block
    steps = per_owner * half
    chunks = tokens // chunk
    total = n * tokens

    z, p = lax.axis_index("zero"), lax.axis_index("peer")
    peers = lax.axis_size("peer")
    side = lax.rem(p, 2)
    base = p - side
    center = half - 1 + side
    worker = (z == half - 1) | (z == half)
    first = worker & (z == center)
    group = base + z - (half - 1)
    z_slot = lax.rem(z, half)
    z_half = lax.div(z, half)

    def at(peer, zero):
        return {"peer": peer, "zero": zero}

    def remote(src, dst, send, recv, peer, zero):
        return pltpu.make_async_remote_copy(
            src_ref=src,
            dst_ref=dst,
            send_sem=send,
            recv_sem=recv,
            device_id=at(peer, zero),
            device_id_type=pl.DeviceIdType.MESH,
        )

    def landed(dst, sem):
        pltpu.make_async_copy(dst, dst, sem).wait()

    def block_of(which, step):
        return which * steps + lax.rem(step, half) * per_owner + lax.div(step, half)

    def span(start, size):
        return pl.ds(pl.multiple_of(start * size, size), size)

    params = [pltpu.make_async_copy(up_in, up, load_sem.at[0])]
    params.append(pltpu.make_async_copy(down_in, down, load_sem.at[1]))
    states = [
        pltpu.make_async_copy(src, dst, load_sem.at[2 + index])
        for index, (src, dst) in enumerate(
            (
                (up_first_in, up_first),
                (down_first_in, down_first),
                (up_second_in, up_second),
                (down_second_in, down_second),
            )
        )
    ]
    for copy in params:
        copy.start()

    barrier = pltpu.get_barrier_semaphore()

    def greet(peer, zero):
        pl.semaphore_signal(
            barrier, inc=1, device_id=at(peer, zero), device_id_type=pl.DeviceIdType.MESH
        )

    for hop in range(1, n):
        for other in range(2):
            greet(base + other, lax.rem(z + hop, n))
    greet(base + 1 - side, z)
    ahead, behind = lax.rem(p + dist, peers), lax.rem(p + peers - dist, peers)
    greet(ahead, z)
    greet(behind, z)
    pl.semaphore_wait(barrier, 2 * n + 1)

    sources, held = (tok_in, out_in), (toks, outs)

    def place(owner, piece):
        return span(owner * chunks + piece, chunk)

    def give(which, piece):
        return remote(
            sources[which].at[span(piece, chunk)],
            held[which].at[place(z, piece)],
            tok_send.at[which, piece],
            tok_recv.at[which, z, piece],
            jnp.where(z == center, base + 1 - side, p),
            center,
        )

    def keep(which, piece):
        return pltpu.make_async_copy(
            sources[which].at[span(piece, chunk)],
            held[which].at[place(z, piece)],
            tok_recv.at[which, z, piece],
        )

    def forward(which, owner, piece):
        spot = held[which].at[place(owner, piece)]
        return remote(
            spot,
            spot,
            fwd_send.at[which, owner, piece],
            tok_recv.at[which, owner, piece],
            base + 1 - side,
            z,
        )

    for piece in range(chunks):
        for which in range(2):
            give(which, piece).start()

            @pl.when(first)
            def _():
                keep(which, piece).start()

    for copy in params:
        copy.wait()
    for copy in states:
        copy.start()

    def give_up(which, step):
        index = which * steps + step
        src, dst = up_stage.at[index], up_cols.at[step, span(z, rows)]
        own = partial(pltpu.make_async_copy, src, dst, upw_recv.at[step, z])
        sent = partial(
            remote, src, dst, upw_send.at[which, step], upw_recv.at[step, z], base + which, center
        )
        return own, sent, (z == center) & (side == which)

    def give_down(piece):
        step = piece * half + z_slot
        src, dst = down_stage.at[piece], down_rows.at[step]
        own = partial(pltpu.make_async_copy, src, dst, downw_recv.at[step])
        sent = partial(
            remote, src, dst, downw_send.at[piece], downw_recv.at[step], base + z_half, center
        )
        return own, sent, (z == center) & (side == z_half)

    def begin(copies):
        own, sent, mine = copies

        @pl.when(mine)
        def _():
            own().start()

        @pl.when(jnp.logical_not(mine))
        def _():
            sent().start()

    def finish_send(copies):
        _, sent, mine = copies

        @pl.when(jnp.logical_not(mine))
        def _():
            sent().wait_send()

    for step in range(steps):
        for which in range(2):
            block = which * steps + (step % half) * per_owner + step // half
            up_stage[which * steps + step] = up[
                :, block * unit_block : (block + 1) * unit_block
            ].astype(BF16)
            begin(give_up(which, step))
        if step % half == 0:
            piece = step // half
            down_stage[piece] = down[piece * unit_block : (piece + 1) * unit_block].astype(BF16)

        @pl.when(z_slot == step % half)
        def _():
            begin(give_down(step // half))

    @pl.when(worker)
    def _():
        @pl.loop(0, chunks)
        def _(piece):
            @pl.loop(0, n)
            def _(owner):
                spot = place(owner, piece)
                for which in range(2):
                    landed(held[which].at[spot], tok_recv.at[which, owner, piece])

                    @pl.when(first & (owner != z))
                    def _():
                        forward(which, owner, piece).start()

                wide = toks[spot, :].astype(F32)
                mean = jnp.mean(wide, axis=1, keepdims=True)
                wide = wide - mean
                spread = jnp.mean(wide * wide, axis=1, keepdims=True)
                wide = wide * lax.rsqrt(spread + 1e-05)
                normed[spot, :] = wide.astype(BF16)
                normed_t[:, spot] = wide.T.astype(BF16)

    tile = min(total, 256)

    def give_grads(step, owner):
        src, dst = up_grad.at[step, span(owner, rows)], up_got.at[side * steps + step]
        own = partial(pltpu.make_async_copy, src, dst, upg_recv.at[side, step])
        sent = partial(
            remote, src, dst, upg_send.at[step, owner], upg_recv.at[side, step], group, owner
        )
        return own, sent, first & (owner == z)

    def give_down_grads(step):
        owner = side * half + lax.rem(step, half)
        piece = lax.div(step, half)
        src, dst = down_grad.at[step], down_got.at[piece]
        own = partial(pltpu.make_async_copy, src, dst, downg_recv.at[piece])
        sent = partial(
            remote, src, dst, downg_send.at[step], downg_recv.at[piece], group, owner
        )
        return own, sent, first & (owner == z)

    def spread_grads(step, far):
        for slot in range(half):
            owner = jnp.where((z_half == 0) != far, slot, half + slot)
            begin(give_grads(step, owner))

        @pl.when((side == z_half) != far)
        def _():
            begin(give_down_grads(step))

    def compute(step):
        for owner in range(n):
            landed(up_cols.at[step, pl.ds(owner * rows, rows)], upw_recv.at[step, owner])
        landed(down_rows.at[step], downw_recv.at[step])

        @pl.when(step == steps - 1)
        def _():
            @pl.loop(EARLY, steps - 1)
            def _(late):
                spread_grads(late, True)

        @pl.loop(0, total // tile)
        def _(index):
            part = span(index, tile)
            pre = jnp.dot(normed[part, :], up_cols[step], preferred_element_type=F32)
            act_grad = lax.dot_general(
                outs[part, :], down_rows[step], (((1,), (1,)), ((), ())), preferred_element_type=F32
            )
            square = pre * pre
            bend = jnp.tanh(pre * (0.7978845608 + (0.7978845608 * 0.044715) * square))
            lift = 0.5 + 0.5 * bend
            slope = lift + (0.5 * pre) * (1.0 - bend * bend) * (
                0.7978845608 + (3.0 * 0.7978845608 * 0.044715) * square
            )
            act_t[:, part] = (pre * lift).T.astype(BF16)
            pre_grad[part, :] = (act_grad * slope).astype(BF16)

        @pl.loop(0, width // unit_block)
        def _(index):
            part = span(index, unit_block)
            down_grad[step, :, part] = jnp.dot(
                act_t[...], outs[:, part], preferred_element_type=F32
            ).astype(BF16)
            up_grad[step, part, :] = jnp.dot(
                normed_t[part, :], pre_grad[...], preferred_element_type=F32
            ).astype(BF16)

        spread_grads(step, False)

        @pl.when((step < EARLY) | (step == steps - 1))
        def _():
            spread_grads(step, True)

    first_scale, second_scale = fixes[0], fixes[1]

    def adam(param, first_ref, second_ref, got, mine, window, piece_window):
        grad = got[piece_window].astype(F32)
        first_new = 0.9 * first_ref[window] + 0.1 * grad
        second_new = 0.999 * second_ref[window] + 0.001 * grad * grad
        first_ref[window] = first_new
        second_ref[window] = second_new
        local = param[window] - (first_new * first_scale) / (
            jnp.sqrt(second_new * second_scale) + 1e-08
        )
        param[window] = local
        mine[piece_window] = local.astype(BF16)

    up_tile, down_tile = min(rows, 32), min(unit_block, 16)

    def pass_up(which, step):
        index = which * steps + step
        return remote(
            up_mine.at[index],
            up_other.at[index],
            upl_send.at[which, step],
            upl_recv.at[which, step],
            behind,
            z,
        )

    def pass_down(piece):
        return remote(
            down_mine.at[piece],
            down_other.at[piece],
            downl_send.at[piece],
            downl_recv.at[piece],
            behind,
            z,
        )

    def update(step):
        for which in range(2):
            index = which * steps + step
            columns = span(block_of(which, step), unit_block)
            landed(up_got.at[index], upg_recv.at[which, step])

            @pl.loop(0, rows // up_tile)
            def _(part):
                some = span(part, up_tile)
                adam(
                    up, up_first, up_second, up_got, up_mine, (some, columns), (index, some)
                )

            pass_up(which, step).start()

        @pl.when(lax.rem(step, half) == z_slot)
        def _():
            piece = lax.div(step, half)
            landed(down_got.at[piece], downg_recv.at[piece])

            @pl.loop(0, unit_block // down_tile)
            def _(part):
                some = span(part, down_tile)
                window = span(piece * (unit_block // down_tile) + part, down_tile)
                adam(
                    down, down_first, down_second, down_got, down_mine, (window,), (piece, some)
                )

            pass_down(piece).start()

    def average(step):
        for which in range(2):
            index = which * steps + step
            columns = span(block_of(which, step), unit_block)
            landed(up_other.at[index], upl_recv.at[which, step])
            up[:, columns] = 0.5 * (up[:, columns] + up_other[index].astype(F32))

        @pl.when(lax.rem(step, half) == z_slot)
        def _():
            piece = lax.div(step, half)
            landed(down_other.at[piece], downl_recv.at[piece])
            window = span(piece, unit_block)
            down[window, :] = 0.5 * (down[window, :] + down_other[piece].astype(F32))

    for copy in states:
        copy.wait()
    delay = jnp.where(worker, jnp.where(first, 1, steps), 0)

    @pl.loop(0, 2 * steps)
    def _(turn):
        @pl.when(worker & (turn < steps))
        def _():
            compute(turn)

        @pl.when((turn >= delay) & (turn < delay + steps))
        def _():
            update(turn - delay)

    @pl.loop(0, steps)
    def _(step):
        average(step)

    for piece in range(chunks):
        for which in range(2):
            give(which, piece).wait_send()

    @pl.when(first)
    def _():
        @pl.loop(0, chunks)
        def _(piece):
            for which in range(2):

                @pl.loop(0, n)
                def _(owner):
                    @pl.when(owner != z)
                    def _():
                        forward(which, owner, piece).wait_send()

    @pl.loop(0, steps)
    def _(step):
        for which in range(2):
            finish_send(give_up(which, step))
            pass_up(which, step).wait_send()

        @pl.when(z_slot == lax.rem(step, half))
        def _():
            finish_send(give_down(lax.div(step, half)))
            pass_down(lax.div(step, half)).wait_send()

        @pl.when(worker)
        def _():
            for owner in range(n):
                finish_send(give_grads(step, owner))
            finish_send(give_down_grads(step))


def fused_step(dist, name, fixes, tokens, out_grad, params):
    n = lax.axis_size("zero")
    own_tokens, width = tokens.shape
    owned = params[1].shape[0]
    units = owned * n
    rows = width // n
    block = min(owned, 256)
    steps = (owned // block) * (n // 2)
    pieces = owned // block
    chunk = min(own_tokens, 128)
    chunks = own_tokens // chunk
    total = n * own_tokens
    dims = (n, own_tokens, width, units, block, chunk)
    hbm = pl.BlockSpec(memory_space=pltpu.HBM)
    vmem = pl.BlockSpec(memory_space=pltpu.VMEM)
    dma = pltpu.SemaphoreType.DMA
    up_shape = jax.ShapeDtypeStruct((rows, units), F32)
    down_shape = jax.ShapeDtypeStruct((owned, width), F32)
    return pl.pallas_call(
        partial(step_kernel, dist, dims),
        out_shape=(up_shape, down_shape) * 3,
        in_specs=[pl.BlockSpec(memory_space=pltpu.SMEM)] + [hbm] * 8,
        out_specs=(vmem,) * 6,
        scratch_shapes=[
            pltpu.VMEM((total, width), BF16),
            pltpu.VMEM((total, width), BF16),
            pltpu.VMEM((total, width), BF16),
            pltpu.VMEM((width, total), BF16),
            pltpu.VMEM((2 * steps, rows, block), BF16),
            pltpu.VMEM((pieces, block, width), BF16),
            pltpu.VMEM((steps, width, block), BF16),
            pltpu.VMEM((steps, block, width), BF16),
            pltpu.VMEM((block, total), BF16),
            pltpu.VMEM((total, block), BF16),
            pltpu.VMEM((steps, width, block), BF16),
            pltpu.VMEM((steps, block, width), BF16),
            pltpu.VMEM((2 * steps, rows, block), BF16),
            pltpu.VMEM((pieces, block, width), BF16),
            pltpu.VMEM((2 * steps, rows, block), BF16),
            pltpu.VMEM((pieces, block, width), BF16),
            pltpu.VMEM((2 * steps, rows, block), BF16),
            pltpu.VMEM((pieces, block, width), BF16),
            dma((6,)),
            dma((2, chunks)),
            dma((2, n, chunks)),
            dma((2, n, chunks)),
            dma((2, steps)),
            dma((steps, n)),
            dma((pieces,)),
            dma((steps,)),
            dma((steps, n)),
            dma((2, steps)),
            dma((steps,)),
            dma((pieces,)),
            dma((2, steps)),
            dma((2, steps)),
            dma((pieces,)),
            dma((pieces,)),
        ],
        compiler_params=pltpu.CompilerParams(
            collective_id=name, has_side_effects=True, vmem_limit_bytes=46 * MIB
        ),
    )(fixes, tokens, out_grad, *params)


def body(
    tokens, out_grad, step, up_param, down_param, up_first, down_first, up_second, down_second
):
    count = (step[0] + 1).astype(F32)
    first_fix = 1.0 - jnp.power(F32(0.9), count)
    second_fix = 1.0 - jnp.power(F32(0.999), count)
    fixes = jnp.stack([0.01 / first_fix, 1.0 / second_fix])
    params = (up_param, down_param, up_first, down_first, up_second, down_second)
    operands = (fixes, tokens[0], out_grad[0], tuple(array[0] for array in params))
    levels = lax.axis_size("peer").bit_length() - 1
    branches = [
        lambda args, level=level: fused_step(2**level, level, *args) for level in range(levels)
    ]
    results = lax.switch(step[0] % levels, branches, operands)
    return tuple(array[None] for array in results)


def solution(mesh):
    spec = P("peer", "zero", None)
    return jax.shard_map(
        body,
        mesh=mesh,
        in_specs=(spec, spec, P()) + (spec,) * 6,
        out_specs=(spec,) * 6,
        check_vma=False,
    )
```

profile of v0, /device:TPU:24, one launch (start us, length us, event | category | flops | bytes accessed | tf_op | source)
XLA Modules:
  0.0 158.0 jit_solution(16284767297087016345)
XLA Ops:
  1.5 0.1 pad_maximum_fusion
  1.5 148.5 %conditional.1 = ((f32[256,2048]{1,0:T(8,128)S(1)}, f32[512,1024]{1,0:T(8,128)S(1)}, f32[256,2048]{1,0:T(8,128)S(1)}, f32[512,1024]{1,0:T(8,128)S(1)}, f32[256,2...) conditional(s32[]{:T(128)} %clamp.3, (bf16[1,512,1024]{2,1,0:T(8,128)(2,1)}, ...), branch_computations={%region_0.1_spmd, %region_1.2_spmd, %region_2.3_spmd} | conditional | bytes 8 | solution.py:544
  1.5 148.5 %branch_0_fun.1 = (f32[256,2048]{1,0:T(8,128)S(1)}, f32[512,1024]{1,0:T(8,128)S(1)}, f32[256,2048]{1,0:T(8,128)S(1)}, f32[512,1024]{1,0:T(8,128)S(1)}, f32[256,2048]{1,0:T(8,128)S(1)}, /*index=5*/f32[512,1024]{1,0:T(8,128)S(1)}) custom-call(f32[2]{0:T(128)S(1)} %get-tuple-element.102.fixes, bf16[512,1024]{1,0:T(8,128)(2,1)} %bitcast.49, ...), custom_call_target="tpu_custom_call" | custom-call | tf_op jit(solution)/shard_map/cond/branch_0_fun/pallas_call | solution.py:484
  150.1 1.3 copy.40
  151.4 1.3 copy.41
  152.7 1.3 copy.42
  154.0 1.3 copy.43
  155.4 1.3 copy.44
  156.7 1.3 copy.45
where the time goes:
time: 160 us; the launch traced here: 158 us
  Pallas kernels  149 us (93%)
  local copies, waits for them, and re-layouts  7.91 us (5%)
    pallas_call x1, Pallas kernels, fused_step(): pl.pallas_call(partial(step_kernel, dist, dims), out_shape=(up_shape, dow...  149 us
    unnamed x6, local copies, waits for them, and re-layouts  7.91 us

commit v1 on v0

--- a/solution.py
+++ b/solution.py
@@ -10,6 +10,7 @@
 MIB = 2**20
 BF16, F32 = jnp.bfloat16, jnp.float32
 EARLY = 1
+STRIP = 64
 
 
 def step_kernel(
@@ -65,13 +66,14 @@
     downl_send,
     downl_recv,
 ):
-    n, tokens, width, units, unit_block, chunk = dims
+    n, tokens, width, units, unit_block, chunk, strip = dims
     half = n // 2
     rows = width // n
     owned = units // n
     per_owner = owned // unit_block
     steps = per_owner * half
     chunks = tokens // chunk
+    strips = unit_block // strip
     total = n * tokens
 
     z, p = lax.axis_index("zero"), lax.axis_index("peer")
@@ -268,13 +270,14 @@
         )
         return own, sent, first & (owner == z)
 
-    def give_down_grads(step):
+    def give_down_grads(step, part):
         owner = side * half + lax.rem(step, half)
         piece = lax.div(step, half)
-        src, dst = down_grad.at[step], down_got.at[piece]
-        own = partial(pltpu.make_async_copy, src, dst, downg_recv.at[piece])
+        some = span(part, strip)
+        src, dst = down_grad.at[step, some], down_got.at[piece, some]
+        own = partial(pltpu.make_async_copy, src, dst, downg_recv.at[piece, part])
         sent = partial(
-            remote, src, dst, downg_send.at[step], downg_recv.at[piece], group, owner
+            remote, src, dst, downg_send.at[step, part], downg_recv.at[piece, part], group, owner
         )
         return own, sent, first & (owner == z)
 
@@ -285,7 +288,9 @@
 
         @pl.when((side == z_half) != far)
         def _():
-            begin(give_down_grads(step))
+            @pl.loop(0, strips)
+            def _(part):
+                begin(give_down_grads(step, part))
 
     def compute(step):
         for owner in range(n):
@@ -344,7 +349,7 @@
         param[window] = local
         mine[piece_window] = local.astype(BF16)
 
-    up_tile, down_tile = min(rows, 32), min(unit_block, 16)
+    up_tile, down_tile = min(rows, 32), min(strip, 16)
 
     def pass_up(which, step):
         index = which * steps + step
@@ -357,12 +362,13 @@
             z,
         )
 
-    def pass_down(piece):
+    def pass_down(piece, part):
+        some = span(part, strip)
         return remote(
-            down_mine.at[piece],
-            down_other.at[piece],
-            downl_send.at[piece],
-            downl_recv.at[piece],
+            down_mine.at[piece, some],
+            down_other.at[piece, some],
+            downl_send.at[piece, part],
+            downl_recv.at[piece, part],
             behind,
             z,
         )
@@ -385,17 +391,27 @@
         @pl.when(lax.rem(step, half) == z_slot)
         def _():
             piece = lax.div(step, half)
-            landed(down_got.at[piece], downg_recv.at[piece])
-
-            @pl.loop(0, unit_block // down_tile)
+
+            @pl.loop(0, strips)
             def _(part):
-                some = span(part, down_tile)
-                window = span(piece * (unit_block // down_tile) + part, down_tile)
-                adam(
-                    down, down_first, down_second, down_got, down_mine, (window,), (piece, some)
-                )
-
-            pass_down(piece).start()
+                landed(down_got.at[piece, span(part, strip)], downg_recv.at[piece, part])
+
+                @pl.loop(0, strip // down_tile)
+                def _(line):
+                    index = part * (strip // down_tile) + line
+                    some = span(index, down_tile)
+                    window = span(piece * (unit_block // down_tile) + index, down_tile)
+                    adam(
+                        down,
+                        down_first,
+                        down_second,
+                        down_got,
+                        down_mine,
+                        (window,),
+                        (piece, some),
+                    )
+
+                pass_down(piece, part).start()
 
     def average(step):
         for which in range(2):
@@ -407,15 +423,20 @@
         @pl.when(lax.rem(step, half) == z_slot)
         def _():
             piece = lax.div(step, half)
-            landed(down_other.at[piece], downl_recv.at[piece])
-            window = span(piece, unit_block)
-            down[window, :] = 0.5 * (down[window, :] + down_other[piece].astype(F32))
+
+            @pl.loop(0, strips)
+            def _(part):
+                some = span(part, strip)
+                landed(down_other.at[piece, some], downl_recv.at[piece, part])
+                window = span(piece * strips + part, strip)
+                down[window, :] = 0.5 * (down[window, :] + down_other[piece, some].astype(F32))
 
     for copy in states:
         copy.wait()
     delay = jnp.where(worker, jnp.where(first, 1, steps), 0)
-
-    @pl.loop(0, 2 * steps)
+    later = jnp.where(worker, steps + 1, 1)
+
+    @pl.loop(0, 2 * steps + 1)
     def _(turn):
         @pl.when(worker & (turn < steps))
         def _():
@@ -425,9 +446,9 @@
         def _():
             update(turn - delay)
 
-    @pl.loop(0, steps)
-    def _(step):
-        average(step)
+        @pl.when((turn >= later) & (turn < later + steps))
+        def _():
+            average(turn - later)
 
     for piece in range(chunks):
         for which in range(2):
@@ -454,13 +475,19 @@
         @pl.when(z_slot == lax.rem(step, half))
         def _():
             finish_send(give_down(lax.div(step, half)))
-            pass_down(lax.div(step, half)).wait_send()
+
+            @pl.loop(0, strips)
+            def _(part):
+                pass_down(lax.div(step, half), part).wait_send()
 
         @pl.when(worker)
         def _():
             for owner in range(n):
                 finish_send(give_grads(step, owner))
-            finish_send(give_down_grads(step))
+
+            @pl.loop(0, strips)
+            def _(part):
+                finish_send(give_down_grads(step, part))
 
 
 def fused_step(dist, name, fixes, tokens, out_grad, params):
@@ -475,12 +502,14 @@
     chunk = min(own_tokens, 128)
     chunks = own_tokens // chunk
     total = n * own_tokens
-    dims = (n, own_tokens, width, units, block, chunk)
+    strip = min(block, STRIP)
+    strips = block // strip
+    dims = (n, own_tokens, width, units, block, chunk, strip)
     hbm = pl.BlockSpec(memory_space=pltpu.HBM)
     vmem = pl.BlockSpec(memory_space=pltpu.VMEM)
     dma = pltpu.SemaphoreType.DMA
-    up_shape = jax.ShapeDtypeStruct((rows, units), F32)
-    down_shape = jax.ShapeDtypeStruct((owned, width), F32)
+    up_shape = pltpu.VMEM((rows, units), F32)
+    down_shape = pltpu.VMEM((owned, width), F32)
     return pl.pallas_call(
         partial(step_kernel, dist, dims),
         out_shape=(up_shape, down_shape) * 3,
@@ -515,17 +544,42 @@
             dma((steps,)),
             dma((steps, n)),
             dma((2, steps)),
-            dma((steps,)),
-            dma((pieces,)),
+            dma((steps, strips)),
+            dma((pieces, strips)),
             dma((2, steps)),
             dma((2, steps)),
-            dma((pieces,)),
-            dma((pieces,)),
+            dma((pieces, strips)),
+            dma((pieces, strips)),
         ],
         compiler_params=pltpu.CompilerParams(
             collective_id=name, has_side_effects=True, vmem_limit_bytes=46 * MIB
         ),
     )(fixes, tokens, out_grad, *params)
+
+
+def store_kernel(*refs):
+    count = len(refs) // 2
+    sems = refs[-1]
+    copies = [
+        pltpu.make_async_copy(refs[index], refs[count + index], sems.at[index])
+        for index in range(count)
+    ]
+    for copy in copies:
+        copy.start()
+    for copy in copies:
+        copy.wait()
+
+
+def store(arrays):
+    return pl.pallas_call(
+        store_kernel,
+        out_shape=tuple(jax.ShapeDtypeStruct(array.shape, array.dtype) for array in arrays),
+        in_specs=[pl.BlockSpec(memory_space=pl.ANY)] * len(arrays),
+        out_specs=(pl.BlockSpec(memory_space=pltpu.HBM),) * len(arrays),
+        scratch_shapes=[pltpu.SemaphoreType.DMA((len(arrays),))],
+        cost_estimate=pl.CostEstimate(flops=10**8, bytes_accessed=24 * MIB, transcendentals=0),
+        compiler_params=pltpu.CompilerParams(vmem_limit_bytes=1 * MIB),
+    )(*arrays)
 
 
 def body(
@@ -539,7 +593,8 @@
     operands = (fixes, tokens[0], out_grad[0], tuple(array[0] for array in params))
     levels = lax.axis_size("peer").bit_length() - 1
     branches = [
-        lambda args, level=level: fused_step(2**level, level, *args) for level in range(levels)
+        lambda args, level=level: store(fused_step(2**level, level, *args))
+        for level in range(levels)
     ]
     results = lax.switch(step[0] % levels, branches, operands)
     return tuple(array[None] for array in results)

time: 160 us -> 153 us (0.956)
  local copies, waits for them, and re-layouts: 7.91 us -> 0 us
  Pallas kernels: 149 us -> 151 us
    unnamed x6 -> x0, local copies, waits for them, and re-layouts: 7.91 us -> none
    pallas_call x0 -> x1, Pallas kernels: none -> 4.65 us  [store(): pl.pallas_call(store_kernel, out_shape=tuple((jax.ShapeDtypeStruct(array....]
    pallas_call x1, Pallas kernels: 149 us -> 146 us  [fused_step(): pl.pallas_call(partial(step_kernel, dist, dims), out_shape=(up_shape, dow...]
where the time goes in v1:
time: 153 us; the launch traced here: 152 us
  Pallas kernels  151 us (99%)
    pallas_call x1, Pallas kernels, fused_step(): pl.pallas_call(partial(step_kernel, dist, dims), out_shape=(up_shape, dow...  146 us
    pallas_call x1, Pallas kernels, store(): pl.pallas_call(store_kernel, out_shape=tuple((jax.ShapeDtypeStruct(array....  4.65 us

profile of v1, /device:TPU:24, one launch (start us, length us, event | category | flops | bytes accessed | tf_op | source)
XLA Modules:
  0.0 152.4 jit_solution(15577137644951516078)
XLA Ops:
  1.5 0.1 pad_maximum_fusion
  1.5 150.9 %conditional.1 = ((f32[256,2048]{1,0:T(8,128)}, f32[512,1024]{1,0:T(8,128)}, f32[256,2048]{1,0:T(8,128)}, f32[512,1024]{1,0:T(8,128)}, f32[256,2048]{1,0:T(8,128)}, /*index=5*/f32[512,1024]{1,0:T(8,128)})) conditional(s32[]{:T(128)} %clamp.3, (bf16[1,512,1024]{2,1,0:T(8,128)(2,1)}, bf16[1,512,1024]{2,1,0:T(8,128)(2,1)}, ...), branch_computations={%region_0.1_spmd.clone, %region_1.2_spmd.clone, %region_2.3_spmd.c... | conditional | flops 100000000 | bytes 25165832 | solution.py:599
  1.5 146.2 %branch_1_fun.2 = (f32[256,2048]{1,0:T(8,128)S(1)}, f32[512,1024]{1,0:T(8,128)S(1)}, f32[256,2048]{1,0:T(8,128)S(1)}, f32[512,1024]{1,0:T(8,128)S(1)}, f32[256,2048]{1,0:T(8,128)S(1)}, /*index=5*/f32[512,1024]{1,0:T(8,128)S(1)}) custom-call(f32[2]{0:T(128)S(1)} %get-tuple-element.195.fixes, bf16[512,1024]{1,0:T(8,128)(2,1)} %bitcast.50, ...), custom_call_target="tpu_custom_call" | custom-call | tf_op jit(solution)/shard_map/cond/branch_1_fun/pallas_call | solution.py:513
  147.8 4.6 %branch_1_fun.3 = (f32[256,2048]{1,0:T(8,128)}, f32[512,1024]{1,0:T(8,128)}, f32[256,2048]{1,0:T(8,128)}, f32[512,1024]{1,0:T(8,128)}, f32[256,2048]{1,0:T(8,128)}, /*index=5*/f32[512,1024]{1,0:T(8,128)}) custom-call(f32[256,2048]{1,0:T(8,128)S(1)} %get-tuple-element.204.refs_0_, f32[512,1024]{1,0:T(8,128)S(1)} %get-tuple-element.205.refs_1_, ...), custom_call_target="tpu_custom_call" | custom-call | flops 100000000 | bytes 25165824 | tf_op jit(solution)/shard_map/cond/branch_1_fun/pallas_call | solution.py:574

commit v2 on v1

v2 whole, which is shorter than its diff:
```python
from functools import partial

import jax
import jax.numpy as jnp
from jax import lax
from jax.experimental import pallas as pl
from jax.experimental.pallas import tpu as pltpu
from jax.sharding import PartitionSpec as P

MIB = 2**20
BF16, F32 = jnp.bfloat16, jnp.float32
EARLY = 1
CHUNK = 256


def step_kernel(
    dist,
    dims,
    fixes,
    tok_in,
    out_in,
    up_in,
    down_in,
    up_first_in,
    down_first_in,
    up_second_in,
    down_second_in,
    up,
    down,
    up_first,
    down_first,
    up_second,
    down_second,
    head,
    held,
    normed,
    normed_t,
    up_stage,
    down_stage,
    up_cols,
    down_rows,
    act_t,
    pre_grad,
    up_grad,
    down_grad,
    up_got,
    down_got,
    up_mine,
    down_mine,
    up_other,
    down_other,
    load_sem,
    tok_send,
    tok_recv,
    fwd_send,
    upw_send,
    upw_recv,
    downw_send,
    downw_recv,
    upg_send,
    upg_recv,
    downg_send,
    downg_recv,
    upl_send,
    upl_recv,
    downl_send,
    downl_recv,
):
    n, tokens, width, units, unit_block, chunk, coarse, fine = dims
    half = n // 2
    rows = width // n
    owned = units // n
    per_owner = owned // unit_block
    steps = per_owner * half
    chunks = tokens // chunk
    total = n * tokens

    z, p = lax.axis_index("zero"), lax.axis_index("peer")
    peers = lax.axis_size("peer")
    side = lax.rem(p, 2)
    base = p - side
    center = half - 1 + side
    worker = (z == half - 1) | (z == half)
    first = worker & (z == center)
    group = base + z - (half - 1)
    z_slot = lax.rem(z, half)
    z_half = lax.div(z, half)

    def at(peer, zero):
        return {"peer": peer, "zero": zero}

    def remote(src, dst, send, recv, peer, zero):
        return pltpu.make_async_remote_copy(
            src_ref=src,
            dst_ref=dst,
            send_sem=send,
            recv_sem=recv,
            device_id=at(peer, zero),
            device_id_type=pl.DeviceIdType.MESH,
        )

    def landed(dst, sem):
        pltpu.make_async_copy(dst, dst, sem).wait()

    def block_of(which, step):
        return which * steps + lax.rem(step, half) * per_owner + lax.div(step, half)

    def span(start, size):
        return pl.ds(pl.multiple_of(start * size, size), size)

    barrier = pltpu.get_barrier_semaphore()

    def greet(peer, zero):
        pl.semaphore_signal(
            barrier, inc=1, device_id=at(peer, zero), device_id_type=pl.DeviceIdType.MESH
        )

    ahead, behind = lax.rem(p + dist, peers), lax.rem(p + peers - dist, peers)
    for other in range(2):

        @pl.when((z != center) | (side != other))
        def _():
            greet(base + other, center)

    for owner in range(n):

        @pl.when(worker & ((group != p) | (z != owner)))
        def _():
            greet(group, owner)

    greet(ahead, z)
    greet(behind, z)

    heads = [
        pltpu.make_async_copy(src.at[pl.ds(0, chunk)], head.at[which], load_sem.at[6 + which])
        for which, src in enumerate((tok_in, out_in))
    ]
    for copy in heads:
        copy.start()
    params = [pltpu.make_async_copy(up_in, up, load_sem.at[0])]
    params.append(pltpu.make_async_copy(down_in, down, load_sem.at[1]))
    states = [
        pltpu.make_async_copy(src, dst, load_sem.at[2 + index])
        for index, (src, dst) in enumerate(
            (
                (up_first_in, up_first),
                (down_first_in, down_first),
                (up_second_in, up_second),
                (down_second_in, down_second),
            )
        )
    ]
    for copy in params:
        copy.start()
    for copy in heads:
        copy.wait()

    once = jnp.where(first, 1, 0)
    pl.semaphore_wait(barrier, 4 - once + jnp.where(worker, n - once, 0))

    sources = (tok_in, out_in)

    def place(owner, piece):
        return span(owner * chunks + piece, chunk)

    def give(which, piece):
        return remote(
            sources[which].at[span(piece, chunk)] if piece else head.at[which],
            held.at[which, place(z, piece)],
            tok_send.at[0],
            tok_recv.at[z, piece],
            jnp.where(z == center, base + 1 - side, p),
            center,
        )

    def keep(which, piece):
        return pltpu.make_async_copy(
            sources[which].at[span(piece, chunk)],
            held.at[which, place(z, piece)],
            tok_recv.at[z, piece],
        )

    def forward(owner, piece):
        spot = held.at[:, place(owner, piece)]
        return remote(
            spot, spot, fwd_send.at[0], tok_recv.at[owner, piece], base + 1 - side, z
        )

    for piece in range(chunks):
        for which in range(2):
            give(which, piece).start()

            @pl.when(first)
            def _():
                keep(which, piece).start()

    for copy in params:
        copy.wait()
    for copy in states:
        copy.start()

    def give_up(which, step):
        index = which * steps + step
        src, dst = up_stage.at[index], up_cols.at[step, span(z, rows)]
        own = partial(pltpu.make_async_copy, src, dst, upw_recv.at[step])
        sent = partial(
            remote, src, dst, upw_send.at[which], upw_recv.at[step], base + which, center
        )
        return own, sent, (z == center) & (side == which)

    def give_down(piece):
        step = piece * half + z_slot
        src, dst = down_stage.at[piece], down_rows.at[step]
        own = partial(pltpu.make_async_copy, src, dst, downw_recv.at[step])
        sent = partial(
            remote, src, dst, downw_send.at[0], downw_recv.at[step], base + z_half, center
        )
        return own, sent, (z == center) & (side == z_half)

    def begin(copies):
        own, sent, mine = copies

        @pl.when(mine)
        def _():
            own().start()

        @pl.when(jnp.logical_not(mine))
        def _():
            sent().start()

    def finish_send(copies):
        _, sent, mine = copies

        @pl.when(jnp.logical_not(mine))
        def _():
            sent().wait_send()

    for step in range(steps):
        for which in range(2):
            block = which * steps + (step % half) * per_owner + step // half
            up_stage[which * steps + step] = up[
                :, block * unit_block : (block + 1) * unit_block
            ].astype(BF16)
            begin(give_up(which, step))
        if step % half == 0:
            piece = step // half
            down_stage[piece] = down[piece * unit_block : (piece + 1) * unit_block].astype(BF16)

        @pl.when(z_slot == step % half)
        def _():
            begin(give_down(step // half))

    @pl.when(worker)
    def _():
        @pl.loop(0, chunks)
        def _(piece):
            @pl.loop(0, n)
            def _(owner):
                spot = place(owner, piece)
                landed(held.at[:, spot], tok_recv.at[owner, piece])

                @pl.when(first & (owner != z))
                def _():
                    forward(owner, piece).start()

                wide = held[0, spot, :].astype(F32)
                mean = jnp.mean(wide, axis=1, keepdims=True)
                wide = wide - mean
                spread = jnp.mean(wide * wide, axis=1, keepdims=True)
                wide = wide * lax.rsqrt(spread + 1e-05)
                normed[spot, :] = wide.astype(BF16)
                normed_t[:, spot] = wide.T.astype(BF16)

    tile = min(total, 256)

    def give_grads(step, owner):
        src, dst = up_grad.at[step, span(owner, rows)], up_got.at[step, side]
        own = partial(pltpu.make_async_copy, src, dst, upg_recv.at[side, step])
        sent = partial(remote, src, dst, upg_send.at[owner], upg_recv.at[side, step], group, owner)
        return own, sent, first & (owner == z)

    def each_strip(step, act):
        piece = lax.div(step, half)

        @pl.when(step < steps - 1)
        def _():
            start = 0
            for index, size in enumerate(coarse):
                act(piece, piece * len(coarse) + index, start, size)
                start += size

        @pl.when(step == steps - 1)
        def _():
            start = 0
            for index, size in enumerate(fine):
                act(piece, (per_owner - 1) * len(coarse) + index, start, size)
                start += size

    def give_down_grads(step, piece, index, start, size):
        slot = lax.rem(step, half)
        owner = side * half + slot
        some = pl.ds(start, size)
        src, dst = down_grad.at[step, some], down_got.at[piece, some]
        own = partial(pltpu.make_async_copy, src, dst, downg_recv.at[index])
        sent = partial(
            remote, src, dst, downg_send.at[slot], downg_recv.at[index], group, owner
        )
        return own, sent, first & (owner == z)

    def spread_grads(step, far):
        for slot in range(half):
            owner = jnp.where((z_half == 0) != far, slot, half + slot)
            begin(give_grads(step, owner))

        @pl.when((side == z_half) != far)
        def _():
            each_strip(step, lambda *strip: begin(give_down_grads(step, *strip)))

    def compute(step):
        landed(up_cols.at[step], upw_recv.at[step])
        landed(down_rows.at[step], downw_recv.at[step])

        @pl.when(step == steps - 1)
        def _():
            @pl.loop(EARLY, steps - 1)
            def _(late):
                spread_grads(late, True)

        @pl.loop(0, total // tile)
        def _(index):
            part = span(index, tile)
            pre = jnp.dot(normed[part, :], up_cols[step], preferred_element_type=F32)
            act_grad = lax.dot_general(
                held[1, part, :], down_rows[step], (((1,), (1,)), ((), ())), preferred_element_type=F32
            )
            square = pre * pre
            bend = jnp.tanh(pre * (0.7978845608 + (0.7978845608 * 0.044715) * square))
            lift = 0.5 + 0.5 * bend
            slope = lift + (0.5 * pre) * (1.0 - bend * bend) * (
                0.7978845608 + (3.0 * 0.7978845608 * 0.044715) * square
            )
            act_t[:, part] = (pre * lift).T.astype(BF16)
            pre_grad[part, :] = (act_grad * slope).astype(BF16)

        @pl.loop(0, width // unit_block)
        def _(index):
            part = span(index, unit_block)
            down_grad[step, :, part] = jnp.dot(
                act_t[...], held[1, :, part], preferred_element_type=F32
            ).astype(BF16)
            up_grad[step, part, :] = jnp.dot(
                normed_t[part, :], pre_grad[...], preferred_element_type=F32
            ).astype(BF16)

        spread_grads(step, False)

        @pl.when((step < EARLY) | (step == steps - 1))
        def _():
            spread_grads(step, True)

    first_scale, second_scale = fixes[0], fixes[1]

    def adam(param, first_ref, second_ref, got, mine, window, piece_window):
        grad = got[piece_window].astype(F32)
        first_new = 0.9 * first_ref[window] + 0.1 * grad
        second_new = 0.999 * second_ref[window] + 0.001 * grad * grad
        first_ref[window] = first_new
        second_ref[window] = second_new
        local = param[window] - (first_new * first_scale) / (
            jnp.sqrt(second_new * second_scale) + 1e-08
        )
        param[window] = local
        mine[piece_window] = local.astype(BF16)

    up_tile, down_tile = min(rows, 32), 16

    def pass_up(which, step):
        return remote(
            up_mine.at[step, which],
            up_other.at[step, which],
            upl_send.at[0],
            upl_recv.at[step],
            behind,
            z,
        )

    def pass_down(piece, index, start, size):
        some = pl.ds(start, size)
        return remote(
            down_mine.at[piece, some],
            down_other.at[piece, some],
            downl_send.at[0],
            downl_recv.at[index],
            behind,
            z,
        )

    def update_strip(piece, index, start, size):
        landed(down_got.at[piece, pl.ds(start, size)], downg_recv.at[index])

        @pl.loop(0, size // down_tile)
        def _(line):
            place_in = start // down_tile + line
            some = span(place_in, down_tile)
            window = span(piece * (unit_block // down_tile) + place_in, down_tile)
            adam(down, down_first, down_second, down_got, down_mine, (window,), (piece, some))

        pass_down(piece, index, start, size).start()

    def average_strip(piece, index, start, size):
        some = pl.ds(start, size)
        landed(down_other.at[piece, some], downl_recv.at[index])
        window = pl.ds(pl.multiple_of(piece * unit_block + start, down_tile), size)
        down[window, :] = 0.5 * (down[window, :] + down_other[piece, some].astype(F32))

    def update_up(which, step):
        landed(up_got.at[step, which], upg_recv.at[which, step])
        columns = span(block_of(which, step), unit_block)

        @pl.loop(0, rows // up_tile)
        def _(part):
            some = span(part, up_tile)
            adam(up, up_first, up_second, up_got, up_mine, (some, columns), (step, which, some))

        pass_up(which, step).start()

    def update(step):
        @pl.when(step == 0)
        def _():
            update_up(side, step)

        update_up(1 - side, step)

        @pl.when(lax.rem(step, half) == z_slot)
        def _():
            each_strip(step, update_strip)

        @pl.when(step < steps - 1)
        def _():
            update_up(side, step + 1)

    def average(step):
        landed(up_other.at[step], upl_recv.at[step])
        for which in range(2):
            columns = span(block_of(which, step), unit_block)
            up[:, columns] = 0.5 * (up[:, columns] + up_other[step, which].astype(F32))

        @pl.when(lax.rem(step, half) == z_slot)
        def _():
            each_strip(step, average_strip)

    def settle():
        landed(held.at[:, pl.ds(0, tokens)], tok_send.at[0])

        @pl.when(first)
        def _():
            landed(held.at[:, pl.ds(0, (n - 1) * tokens)], fwd_send.at[0])

        for which in range(2):

            @pl.when((z != center) | (side != which))
            def _():
                landed(up_stage.at[pl.ds(which * steps, steps)], upw_send.at[which])

        @pl.when((z != center) | (side != z_half))
        def _():
            landed(down_stage, downw_send.at[0])

    for copy in states:
        copy.wait()
    delay = jnp.where(worker, jnp.where(first, 1, steps), 0)
    later = jnp.where(worker, steps + 1, 1)

    @pl.loop(0, 2 * steps + 1)
    def _(turn):
        @pl.when(worker & (turn < steps))
        def _():
            compute(turn)

        @pl.when(turn == delay + steps - 2)
        def _():
            settle()

        @pl.when((turn >= delay) & (turn < delay + steps))
        def _():
            update(turn - delay)

        @pl.when((turn >= later) & (turn < later + steps))
        def _():
            average(turn - later)

    landed(up_mine, upl_send.at[0])
    landed(down_mine, downl_send.at[0])

    @pl.when(worker)
    def _():
        for owner in range(n):

            @pl.when(jnp.logical_not(first & (z == owner)))
            def _():
                landed(up_grad.at[:, pl.ds(owner * rows, rows)], upg_send.at[owner])

        for slot in range(half):

            @pl.when(jnp.logical_not(first & (z == side * half + slot)))
            def _():
                landed(down_grad.at[pl.ds(slot * per_owner, per_owner)], downg_send.at[slot])


def fused_step(dist, name, fixes, tokens, out_grad, params):
    n = lax.axis_size("zero")
    own_tokens, width = tokens.shape
    owned = params[1].shape[0]
    units = owned * n
    rows = width // n
    block = min(owned, 256)
    steps = (owned // block) * (n // 2)
    pieces = owned // block
    chunk = min(own_tokens, CHUNK)
    chunks = own_tokens // chunk
    total = n * own_tokens
    quarter = block // 4
    coarse, fine = (block // 4,) * 4, (quarter,) * 3 + (quarter // 2,) + (quarter // 4,) * 2
    strips = (pieces - 1) * len(coarse) + len(fine)
    dims = (n, own_tokens, width, units, block, chunk, coarse, fine)
    hbm = pl.BlockSpec(memory_space=pltpu.HBM)
    vmem = pl.BlockSpec(memory_space=pltpu.VMEM)
    dma = pltpu.SemaphoreType.DMA
    up_shape = pltpu.VMEM((rows, units), F32)
    down_shape = pltpu.VMEM((owned, width), F32)
    return pl.pallas_call(
        partial(step_kernel, dist, dims),
        out_shape=(up_shape, down_shape) * 3,
        in_specs=[pl.BlockSpec(memory_space=pltpu.SMEM)] + [hbm] * 8,
        out_specs=(vmem,) * 6,
        scratch_shapes=[
            pltpu.VMEM((2, chunk, width), BF16),
            pltpu.VMEM((2, total, width), BF16),
            pltpu.VMEM((total, width), BF16),
            pltpu.VMEM((width, total), BF16),
            pltpu.VMEM((2 * steps, rows, block), BF16),
            pltpu.VMEM((pieces, block, width), BF16),
            pltpu.VMEM((steps, width, block), BF16),
            pltpu.VMEM((steps, block, width), BF16),
            pltpu.VMEM((block, total), BF16),
            pltpu.VMEM((total, block), BF16),
            pltpu.VMEM((steps, width, block), BF16),
            pltpu.VMEM((steps, block, width), BF16),
            pltpu.VMEM((steps, 2, rows, block), BF16),
            pltpu.VMEM((pieces, block, width), BF16),
            pltpu.VMEM((steps, 2, rows, block), BF16),
            pltpu.VMEM((pieces, block, width), BF16),
            pltpu.VMEM((steps, 2, rows, block), BF16),
            pltpu.VMEM((pieces, block, width), BF16),
            dma((8,)),
            dma((1,)),
            dma((n, chunks)),
            dma((1,)),
            dma((2,)),
            dma((steps,)),
            dma((1,)),
            dma((steps,)),
            dma((n,)),
            dma((2, steps)),
            dma((n // 2,)),
            dma((strips,)),
            dma((1,)),
            dma((steps,)),
            dma((1,)),
            dma((strips,)),
        ],
        compiler_params=pltpu.CompilerParams(
            collective_id=name, has_side_effects=True, vmem_limit_bytes=46 * MIB
        ),
    )(fixes, tokens, out_grad, *params)


def store_kernel(*refs):
    count = len(refs) // 2
    sems = refs[-1]
    copies = [
        pltpu.make_async_copy(refs[index], refs[count + index], sems.at[index])
        for index in range(count)
    ]
    for copy in copies:
        copy.start()
    for copy in copies:
        copy.wait()


def store(arrays):
    return pl.pallas_call(
        store_kernel,
        out_shape=tuple(jax.ShapeDtypeStruct(array.shape, array.dtype) for array in arrays),
        in_specs=[pl.BlockSpec(memory_space=pl.ANY)] * len(arrays),
        out_specs=(pl.BlockSpec(memory_space=pltpu.HBM),) * len(arrays),
        scratch_shapes=[pltpu.SemaphoreType.DMA((len(arrays),))],
        cost_estimate=pl.CostEstimate(flops=10**8, bytes_accessed=24 * MIB, transcendentals=0),
        compiler_params=pltpu.CompilerParams(vmem_limit_bytes=1 * MIB),
    )(*arrays)


def body(
    tokens, out_grad, step, up_param, down_param, up_first, down_first, up_second, down_second
):
    count = (step[0] + 1).astype(F32)
    first_fix = 1.0 - jnp.power(F32(0.9), count)
    second_fix = 1.0 - jnp.power(F32(0.999), count)
    fixes = jnp.stack([0.01 / first_fix, 1.0 / second_fix])
    params = (up_param, down_param, up_first, down_first, up_second, down_second)
    operands = (fixes, tokens[0], out_grad[0], tuple(array[0] for array in params))
    levels = lax.axis_size("peer").bit_length() - 1
    branches = [
        lambda args, level=level: store(fused_step(2**level, level, *args))
        for level in range(levels)
    ]
    results = lax.switch(step[0] % levels, branches, operands)
    return tuple(array[None] for array in results)


def solution(mesh):
    spec = P("peer", "zero", None)
    return jax.shard_map(
        body,
        mesh=mesh,
        in_specs=(spec, spec, P()) + (spec,) * 6,
        out_specs=(spec,) * 6,
        check_vma=False,
    )
```

time: 153 us -> 151 us (0.987)
  Pallas kernels: 151 us -> 149 us
    pallas_call x1, Pallas kernels: 146 us -> 145 us  [fused_step(): pl.pallas_call(partial(step_kernel, dist, dims), out_shape=(up_shape, dow...]
where the time goes in v2:
time: 151 us
  Pallas kernels  149 us (99%)
  between operations  1.64 us (1%)
    pallas_call x1, Pallas kernels, fused_step(): pl.pallas_call(partial(step_kernel, dist, dims), out_shape=(up_shape, dow...  145 us
    pallas_call x1, Pallas kernels, store(): pl.pallas_call(store_kernel, out_shape=tuple((jax.ShapeDtypeStruct(array....  4.65 us

profile of v2, /device:TPU:24, one launch (start us, length us, event | category | flops | bytes accessed | tf_op | source)
XLA Modules:
  0.0 151.3 jit_solution(2916667506368144198)
XLA Ops:
  1.5 0.1 pad_maximum_fusion
  1.5 149.6 %conditional.1 = ((f32[256,2048]{1,0:T(8,128)}, f32[512,1024]{1,0:T(8,128)}, f32[256,2048]{1,0:T(8,128)}, f32[512,1024]{1,0:T(8,128)}, f32[256,2048]{1,0:T(8,128)}, /*index=5*/f32[512,1024]{1,0:T(8,128)})) conditional(s32[]{:T(128)} %clamp.3, (bf16[1,512,1024]{2,1,0:T(8,128)(2,1)}, bf16[1,512,1024]{2,1,0:T(8,128)(2,1)}, ...), branch_computations={%region_0.1_spmd.clone, %region_1.2_spmd.clone, %region_2.3_spmd.c... | conditional | flops 100000000 | bytes 25165832 | solution.py:617
  1.5 144.7 %branch_2_fun.2 = (f32[256,2048]{1,0:T(8,128)S(1)}, f32[512,1024]{1,0:T(8,128)S(1)}, f32[256,2048]{1,0:T(8,128)S(1)}, f32[512,1024]{1,0:T(8,128)S(1)}, f32[256,2048]{1,0:T(8,128)S(1)}, /*index=5*/f32[512,1024]{1,0:T(8,128)S(1)}) custom-call(f32[2]{0:T(128)S(1)} %get-tuple-element.211.fixes, bf16[512,1024]{1,0:T(8,128)(2,1)} %bitcast.51, ...), custom_call_target="tpu_custom_call" | custom-call | tf_op jit(solution)/shard_map/cond/branch_2_fun/pallas_call | solution.py:531
  146.2 4.6 %branch_2_fun.3 = (f32[256,2048]{1,0:T(8,128)}, f32[512,1024]{1,0:T(8,128)}, f32[256,2048]{1,0:T(8,128)}, f32[512,1024]{1,0:T(8,128)}, f32[256,2048]{1,0:T(8,128)}, /*index=5*/f32[512,1024]{1,0:T(8,128)}) custom-call(f32[256,2048]{1,0:T(8,128)S(1)} %get-tuple-element.220.refs_0_, f32[512,1024]{1,0:T(8,128)S(1)} %get-tuple-element.221.refs_1_, ...), custom_call_target="tpu_custom_call" | custom-call | flops 100000000 | bytes 25165824 | tf_op jit(solution)/shard_map/cond/branch_2_fun/pallas_call | solution.py:592

commit v3 on v2

--- a/solution.py
+++ b/solution.py
@@ -152,9 +152,6 @@
     ]
     for copy in params:
         copy.start()
-    for copy in heads:
-        copy.wait()
-
     once = jnp.where(first, 1, 0)
     pl.semaphore_wait(barrier, 4 - once + jnp.where(worker, n - once, 0))
 
@@ -188,10 +185,14 @@
 
     for piece in range(chunks):
         for which in range(2):
+            if piece == 0:
+                heads[which].wait()
             give(which, piece).start()
 
-            @pl.when(first)
-            def _():
+    @pl.when(first)
+    def _():
+        for piece in range(chunks):
+            for which in range(2):
                 keep(which, piece).start()
 
     for copy in params:

time: 151 us -> 151 us (level)
  no operation moved by 1% of the time
where the time goes in v3:
time: 151 us
  Pallas kernels  149 us (99%)
  between operations  1.64 us (1%)
    pallas_call x1, Pallas kernels, fused_step(): pl.pallas_call(partial(step_kernel, dist, dims), out_shape=(up_shape, dow...  145 us
    pallas_call x1, Pallas kernels, store(): pl.pallas_call(store_kernel, out_shape=tuple((jax.ShapeDtypeStruct(array....  4.65 us

profile of v3, /device:TPU:24, one launch (start us, length us, event | category | flops | bytes accessed | tf_op | source)
XLA Modules:
  0.0 151.2 jit_solution(5220020916530432547)
XLA Ops:
  1.5 0.1 pad_maximum_fusion
  1.5 149.5 %conditional.1 = ((f32[256,2048]{1,0:T(8,128)}, f32[512,1024]{1,0:T(8,128)}, f32[256,2048]{1,0:T(8,128)}, f32[512,1024]{1,0:T(8,128)}, f32[256,2048]{1,0:T(8,128)}, /*index=5*/f32[512,1024]{1,0:T(8,128)})) conditional(s32[]{:T(128)} %clamp.3, (bf16[1,512,1024]{2,1,0:T(8,128)(2,1)}, bf16[1,512,1024]{2,1,0:T(8,128)(2,1)}, ...), branch_computations={%region_0.1_spmd.clone, %region_1.2_spmd.clone, %region_2.3_spmd.c... | conditional | flops 100000000 | bytes 25165832 | solution.py:618
  1.5 144.6 %branch_1_fun.2 = (f32[256,2048]{1,0:T(8,128)S(1)}, f32[512,1024]{1,0:T(8,128)S(1)}, f32[256,2048]{1,0:T(8,128)S(1)}, f32[512,1024]{1,0:T(8,128)S(1)}, f32[256,2048]{1,0:T(8,128)S(1)}, /*index=5*/f32[512,1024]{1,0:T(8,128)S(1)}) custom-call(f32[2]{0:T(128)S(1)} %get-tuple-element.195.fixes, bf16[512,1024]{1,0:T(8,128)(2,1)} %bitcast.50, ...), custom_call_target="tpu_custom_call" | custom-call | tf_op jit(solution)/shard_map/cond/branch_1_fun/pallas_call | solution.py:532
  146.2 4.6 %branch_1_fun.3 = (f32[256,2048]{1,0:T(8,128)}, f32[512,1024]{1,0:T(8,128)}, f32[256,2048]{1,0:T(8,128)}, f32[512,1024]{1,0:T(8,128)}, f32[256,2048]{1,0:T(8,128)}, /*index=5*/f32[512,1024]{1,0:T(8,128)}) custom-call(f32[256,2048]{1,0:T(8,128)S(1)} %get-tuple-element.204.refs_0_, f32[512,1024]{1,0:T(8,128)S(1)} %get-tuple-element.205.refs_1_, ...), custom_call_target="tpu_custom_call" | custom-call | flops 100000000 | bytes 25165824 | tf_op jit(solution)/shard_map/cond/branch_1_fun/pallas_call | solution.py:593
